TPU v7x, 32 devices: a whole 2x2x4 slice. The times are simulated.
32 devices in a mesh: shadow: 16 (over z, y, core), vocab: 2 (over x).
Axes of the slice: x: 2, y: 2, z: 4, core: 2. Of those that a mesh axis runs over, the one named last changes fastest.
Arguments:
- hidden: bfloat16 [64, 128, 2048], P('shadow'), may hold values from -18 to 18
- targets: int32 [128], replicated, may hold values from 0 to 4095
- membership: int32 [64, 4], P('shadow'), may hold values from 0 to 1, as said below
- unembedding: bfloat16 [4096, 2048], P(('shadow', 'vocab')), may hold values from -1 to 1
Outputs:
- score: float32 [64, 128], P('shadow', 'vocab')
Inputs may be any that keep to these rules, and one draw needn't show every extreme that they name: `membership`: each candidate sequence is a member of exactly 32 of the shadow models.
All inputs are finite; a program needn't handle non-finite values.
Results may differ from a plain program's by a relative error of at most 0.00055.
Values may be sent and summed in bfloat16 or wider, within the bound.
A program may use at most 64 MiB of HBM per device.

v0:
```python
import jax
import jax.numpy as jnp
from jax import lax
from jax.sharding import PartitionSpec as P

SEQ = 32


NEG_FILL = -1e30
VAR_FLOOR = 0.5


def merged(value, axis, combine):
    everything = jax.tree.map(lambda part: lax.all_gather(part, axis), value)
    first = jax.tree.map(lambda part: part[0], everything)

    def turn(k, so_far):
        return combine(so_far, jax.tree.map(lambda part: part[k], everything))

    return lax.fori_loop(1, lax.axis_size(axis), turn, first)


def start_state(row_count):
    return (
        jnp.full((row_count,), NEG_FILL, jnp.float32),
        jnp.zeros((row_count,), jnp.float32),
        jnp.zeros((row_count,), jnp.float32),
    )


def fold_block(running, flat_rows, wanted, block_rows, vocab_rows):
    highest, summed, target_logit = running
    logits = lax.dot_general(
        flat_rows, block_rows, (((1,), (1,)), ((), ())), preferred_element_type=jnp.float32
    )
    target_hit = wanted[:, None] == vocab_rows[None, :]
    target_logit = jnp.sum(jnp.where(target_hit, logits, 0.0), axis=1)
    others = jnp.where(target_hit, NEG_FILL, logits)
    raised = jnp.maximum(highest, jnp.max(others, axis=1))
    fresh_terms = jnp.where(target_hit, 0.0, jnp.exp(others - raised[:, None]))
    summed = jnp.sum(fresh_terms, axis=1)
    return (raised, summed, target_logit)


def combine_pairs(earlier, latter):
    raised = jnp.maximum(earlier[0], latter[0])
    summed = earlier[1] * jnp.exp(earlier[0] - raised) + latter[1] * jnp.exp(latter[0] - raised)
    return (raised, summed, earlier[2] + latter[2])


def per_device(hidden, targets, membership, unembedding):
    shadow_count, token_count, model_width = hidden.shape
    head_rows = unembedding.shape[0]
    vocab_count = lax.axis_size("vocab")
    vocab_index = lax.axis_index("vocab")
    shadows_total = shadow_count * lax.axis_size("shadow")
    slice_tokens = token_count // vocab_count
    slice_start = vocab_index * slice_tokens
    flat_rows = hidden.reshape(shadow_count * token_count, model_width)
    wanted = jnp.tile(targets, shadow_count)
    block_rows = lax.all_gather(unembedding, "shadow", axis=0, tiled=True)
    gathered = jnp.arange(block_rows.shape[0], dtype=jnp.int32)
    vocab_rows = (
        gathered // head_rows * vocab_count + vocab_index
    ) * head_rows + gathered % head_rows
    highest, summed, target_logit = fold_block(
        start_state(flat_rows.shape[0]), flat_rows, wanted, block_rows, vocab_rows
    )
    highest, summed, target_logit = merged((highest, summed, target_logit), "vocab", combine_pairs)
    all_confidence = (target_logit - (highest + jnp.log(summed))).reshape(shadow_count, token_count)
    confidence = lax.dynamic_slice_in_dim(all_confidence, slice_start, slice_tokens, 1)
    member_tokens = jnp.repeat(membership, SEQ, axis=1)
    outside = (1 - lax.dynamic_slice_in_dim(member_tokens, slice_start, slice_tokens, 1)).astype(
        jnp.float32
    )
    weighted = outside * confidence
    first_moment, second_moment = lax.psum(
        (jnp.sum(weighted, axis=0), jnp.sum(weighted * confidence, axis=0)), "shadow"
    )
    out_count = shadows_total // 2 - outside
    out_mean = (first_moment[None, :] - weighted) / out_count
    out_variance = (
        second_moment[None, :] - weighted * confidence
    ) / out_count - out_mean * out_mean
    return (confidence - out_mean) * lax.rsqrt(jnp.maximum(out_variance, 0.0) + VAR_FLOOR)


def solution(mesh):
    return jax.shard_map(
        per_device,
        mesh=mesh,
        in_specs=(P("shadow", None, None), P(), P("shadow", None), P(("shadow", "vocab"), None)),
        out_specs=P("shadow", "vocab"),
        check_vma=False,
    )
```

profile of v0, /device:TPU:0, one launch (start us, length us, event | category | flops | bytes accessed | tf_op | source)
XLA Modules:
  0.0 145.8 jit_solution(8924204590012393427)
XLA Ops:
  6.5 0.0 copy-start
  6.5 0.0 all-gather.8.cloned.1.call-start
  6.5 0.7 all-gather.8.cloned.1.call-update
  7.3 0.8 broadcast_in_dim.22
  8.0 0.1 reshape.55
  8.1 0.7 broadcast_bitcast_fusion
  8.8 77.8 %all-gather.8.cloned.1.call-done = bf16[2048,2048]{1,0:T(8,128)(2,1)} async-done(((bf16[128,2048]{1,0:T(8,128)(2,1)}), bf16[2048,2048]{1,0:T(8,128)(2,1)}) %all-gather.8.cloned.1.call-update) | async-done | bytes 8388624 | tf_op jit(solution)/shard_map/all_gather | solution.py:61
  86.6 0.0 copy-done
  86.6 7.1 %fusion.2 = (f32[512]{0:T(512)S(1)}, f32[512,2048]{1,0:T(8,128)S(1)}) fusion(s32[2048]{0:T(1024)S(1)} %fusion.12, s32[512]{0:T(512)S(1)} %broadcast_bitcast_fusion, bf16[512,2048]{1,0:T(8,128)(2,1)S(1)} %bitcast.13, bf16[2048,2048]{1,0:T(8,128)(2,1)} %all-gather.8.cloned.1.call-done), kind=kOutput, calls=%fused_computation.5 | convolution fusion | flops 4298112512 | bytes 14692352 | tf_op jit(solution)/shard_map/dot_general | solution.py:33
  93.7 1.9 %fusion.1 = (f32[512]{0:T(512)S(1)}, f32[512]{0:T(512)S(1)}) fusion(f32[512,2048]{1,0:T(8,128)S(1)} %get-tuple-element.40, f32[512]{0:T(512)S(1)} %broadcast_maximum_fusion, s32[2048]{0:T(1024)S(1)} %fusion.12, s32[512]{0:T(512)S(1)} %broadcast_bitcast_fusion), kind=kLoop, calls=%fused_computation.4 | loop fusion | flops 7339008 | bytes 4210688 | tf_op jit(solution)/shard_map/reduce_sum | solution.py:41
  95.6 4.4 %all-gather.4 = f32[2,1,512]{2,1,0:T(1,128)S(1)} all-gather(f32[1,1,512]{2,1,0:T(1,128)S(1)} %bitcast.14), channel_id=3, replica_groups=mesh['shadow'=16,'vocab'=2] {'vocab'}, dimensions={0}, use_global_device_ids=true | all-gather | bytes 6144 | tf_op jit(solution)/shard_map/all_gather | solution.py:14
  99.9 4.4 %all-gather.3 = f32[2,1,512]{2,1,0:T(1,128)S(1)} all-gather(f32[1,1,512]{2,1,0:T(1,128)S(1)} %bitcast.16), channel_id=2, replica_groups=mesh['shadow'=16,'vocab'=2] {'vocab'}, dimensions={0}, use_global_device_ids=true | all-gather | bytes 6144 | tf_op jit(solution)/shard_map/all_gather | solution.py:14
  104.3 4.4 %all-gather.5 = f32[2,1,512]{2,1,0:T(1,128)S(1)} all-gather(f32[1,1,512]{2,1,0:T(1,128)S(1)} %bitcast.15), channel_id=4, replica_groups=mesh['shadow'=16,'vocab'=2] {'vocab'}, dimensions={0}, use_global_device_ids=true | all-gather | bytes 6144 | tf_op jit(solution)/shard_map/all_gather | solution.py:14
  108.7 0.1 fusion.15
  108.8 29.5 %all-reduce = (f32[64]{0:T(128)S(1)}, f32[64]{0:T(128)S(1)}) all-reduce(f32[64]{0:T(128)S(1)} %get-tuple-element.22, f32[64]{0:T(128)S(1)} %get-tuple-element.21), channel_id=1, replica_groups=mesh['shadow'=16,'vocab'=2] {'shadow'}, use_global_device_ids=true, to_apply=%region_6.7 | all-reduce | flops 128 | bytes 1024 | tf_op jit(solution)/shard_map/psum | solution.py:77
  138.3 0.7 rsqrt_multiply_fusion
  (6 shorter events, 0.0 us)
Async XLA Ops:
  6.5 80.0 %copy-start = (bf16[4,128,2048]{2,1,0:T(8,128)(2,1)S(1)}, bf16[4,128,2048]{2,1,0:T(8,128)(2,1)}, u32[]{:S(2)}) copy-start(bf16[4,128,2048]{2,1,0:T(8,128)(2,1)} %param.4) | copy-start | bytes 6291460
  6.5 80.0 %all-gather.8.cloned.1.call-start = ((), (), s32[]{:S(2)}) async-start(), calls=%async_computation | async-start | bytes 8912896 | tf_op jit(solution)/shard_map/all_gather | solution.py:61
Sparse Core Ops, SparseCore 0:
  9.5 77.0 all-gather.7
where the time goes:
time: 146 us
  waiting for transfers between devices  78.5 us (54%)
  blocking collectives  42.6 us (29%)
  between operations  13.4 us (9%)
  matrix products  7.11 us (5%)
  other arithmetic  2.67 us (2%)
  local copies, waits for them, and re-layouts  1.5 us (1%)
    all_gather x1, waiting for transfers between devices, per_device(): block_rows = lax.all_gather(unembedding, 'shadow', axis=0, tiled=True)  77.8 us
    psum x1, blocking collectives, per_device(): lax.psum((jnp.sum(weighted, axis=0), jnp.sum(weighted * confidence, axis=...  29.5 us
    all_gather x3, blocking collectives, merged(): everything = jax.tree.map(lambda part: lax.all_gather(part, axis), value)  13.1 us
    dot_general x1, matrix products, fold_block(): lax.dot_general(flat_rows, block_rows, (((1,), (1,)), ((), ())), preferre...  7.11 us
  transfers between devices with their start and end apart: 1, of which 1 were waited for; matrix products, arithmetic and copies ran while one was open for 1% of the time, Pallas kernels for 0%

commit v1 on v0

v1 whole, which is shorter than its diff:
```python
import functools

import jax
import jax.numpy as jnp
from jax import lax
from jax.experimental import pallas as pl
from jax.experimental.pallas import tpu as pltpu
from jax.sharding import PartitionSpec as P

SEQ = 32
NEG_FILL = -1e30
VAR_FLOOR = 0.5
MESH = pl.DeviceIdType.MESH

HEAD_CHUNKS = 4
HIDDEN_CHUNKS = 8


def kernel(
    nsh,
    nv,
    seq,
    hidden_hbm,
    targets_ref,
    member_ref,
    head_hbm,
    out_ref,
    hid,
    heads,
    top,
    tot,
    tgt,
    stat_send,
    stat_recv,
    mom_send,
    mom_recv,
    load_sem,
    up_send,
    down_send,
    line_recv,
    sib_send,
    sib_recv,
    hy_send,
    hy_recv,
    hx_send,
    hx_recv,
    st_send,
    st_recv,
    mo_send,
    mo_recv,
):
    nz = nsh // 4
    chunks, chunk_rows = heads.shape[1], heads.shape[3]
    head_rows = chunks * chunk_rows
    width = heads.shape[4]
    rows = hid.shape[1]
    tokens = targets_ref.shape[1]
    group = rows // tokens
    piece = rows // nv
    hparts = hy_send.shape[0]
    part = piece // hparts

    me = lax.axis_index("shadow")
    v = lax.axis_index("vocab")
    z, y, c = me // 4, (me // 2) % 2, me % 2
    sibling = me + 1 - 2 * c
    across = me + 2 - 4 * y
    has_up, has_down = z + 1 < nz, z >= 1
    one, zero = jnp.int32(1), jnp.int32(0)

    load_head = [
        pltpu.make_async_copy(
            head_hbm.at[pl.ds(j * chunk_rows, chunk_rows)], heads.at[z, j, c], load_sem.at[j]
        )
        for j in range(chunks)
    ]
    load_hidden = pltpu.make_async_copy(hidden_hbm, hid.at[0], load_sem.at[chunks])
    for copy in load_head:
        copy.start()
    load_hidden.start()

    barrier = pltpu.get_barrier_semaphore()

    def greet(s, w):
        pl.semaphore_signal(barrier, inc=1, device_id=(s, w), device_id_type=MESH)

    greet(sibling, v)
    for d in range(nv):
        if d:
            greet(me, (v + d) % nv)
        greet(across, (v + d) % nv)

    @pl.when(has_up)
    def _():
        greet(me + 4, v)

    @pl.when(has_down)
    def _():
        greet(me - 4, v)

    top[...] = jnp.full_like(top, NEG_FILL)
    tot[...] = jnp.zeros_like(tot)
    tgt[...] = jnp.zeros_like(tgt)
    pl.semaphore_wait(
        barrier, 2 * nv + jnp.where(has_up, one, zero) + jnp.where(has_down, one, zero)
    )

    def line(block, j, send, target):
        return pltpu.make_async_remote_copy(
            src_ref=heads.at[block, j, c],
            dst_ref=heads.at[block, j, c],
            send_sem=send.at[block, j],
            recv_sem=line_recv.at[block, j],
            device_id=(target, v),
            device_id_type=MESH,
        )

    def side(block, j, core):
        return pltpu.make_async_remote_copy(
            src_ref=heads.at[block, j, core],
            dst_ref=heads.at[block, j, core],
            send_sem=sib_send.at[block, j],
            recv_sem=sib_recv.at[block, j],
            device_id=(sibling, v),
            device_id_type=MESH,
        )

    def over_y(i):
        where = pl.ds(pl.multiple_of(v * piece + i * part, part), part)
        return pltpu.make_async_remote_copy(
            src_ref=hid.at[0, where],
            dst_ref=hid.at[1, where],
            send_sem=hy_send.at[i],
            recv_sem=hy_recv.at[i],
            device_id=(across, v),
            device_id_type=MESH,
        )

    def over_x(d, i, owner):
        where = pl.ds(pl.multiple_of(owner * piece + i * part, part), part)
        return pltpu.make_async_remote_copy(
            src_ref=hid.at[1, where],
            dst_ref=hid.at[1, where],
            send_sem=hx_send.at[d - 1, i],
            recv_sem=hx_recv.at[d - 1, i],
            device_id=(me, (v + d) % nv),
            device_id_type=MESH,
        )

    for j in range(chunks):
        load_head[j].wait()

        @pl.when(has_up)
        def _():
            line(z, j, up_send, me + 4).start()

        @pl.when(has_down)
        def _():
            line(z, j, down_send, me - 4).start()

        side(z, j, c).start()
    load_hidden.wait()
    for i in range(hparts):
        over_y(i).start()

    wanted = targets_ref[...]

    def fold(which, words, first, block):
        count = words.shape[0]
        logits = lax.dot_general(
            words, hid[which], (((1,), (1,)), ((), ())), preferred_element_type=jnp.float32
        )
        i = lax.broadcasted_iota(jnp.int32, (count, tokens), 0)
        core = (i // chunk_rows) % 2
        inside = first + i // (2 * chunk_rows) * chunk_rows + i % chunk_rows
        ids = (((block * 2 + y) * 2 + core) * nv + v) * head_rows + inside
        hit = ids == wanted
        for s in range(group):
            row = pl.ds(which * group + s, 1)
            mine = logits[:, s * tokens : (s + 1) * tokens]
            tgt[row] += jnp.sum(jnp.where(hit, mine, 0.0), axis=0, keepdims=True)
            others = jnp.where(hit, NEG_FILL, mine)
            before = top[row]
            raised = jnp.maximum(before, jnp.max(others, axis=0, keepdims=True))
            terms = jnp.sum(jnp.exp(others - raised), axis=0, keepdims=True)
            tot[row] = tot[row] * jnp.exp(before - raised) + terms
            top[row] = raised

    def whole_block(which, block):
        words = heads[block].reshape(2 * head_rows, width)
        fold(which, words, 0, block)

    def one_chunk(which, block, j):
        words = heads[block, j].reshape(2 * chunk_rows, width)
        fold(which, words, j * chunk_rows, block)

    for j in range(chunks):
        side(z, j, 1 - c).wait_recv()
    whole_block(0, z)

    rounds = (nz - 1) * chunks

    def turn(r, _):
        k, j = 1 + r // chunks, r % chunks
        live = r < rounds
        low, high = z - k, z + k

        @pl.when(live & (low >= 0))
        def _():
            line(low, j, up_send, me).wait_recv()

            @pl.when(has_up)
            def _():
                line(low, j, up_send, me + 4).start()

            side(low, j, c).start()

        @pl.when(live & (high < nz))
        def _():
            line(high, j, down_send, me).wait_recv()

            @pl.when(has_down)
            def _():
                line(high, j, down_send, me - 4).start()

            side(high, j, c).start()

        @pl.when(r < hparts)
        def _():
            over_y(r).wait_recv()
            for d in range(1, nv):
                over_x(d, r, v).start()

        q = r - 1
        kq, jq = 1 + (r + chunks - 1) // chunks - 1, (r + chunks - 1) % chunks

        @pl.when(r == rounds - chunks + 1)
        def _():
            for d in range(1, nv):
                for i in range(hparts):
                    over_x(d, i, (v + nv - d) % nv).wait_recv()

            def catch_up(block, _):
                away = jnp.where(block > z, block - z, z - block)

                @pl.when(away < nz - 1)
                def _():
                    whole_block(1, block)

                return 0

            lax.fori_loop(0, nz, catch_up, 0)

        def use(block):
            side(block, jq, 1 - c).wait_recv()
            one_chunk(0, block, jq)

            @pl.when(kq == nz - 1)
            def _():
                one_chunk(1, block, jq)

        @pl.when((q >= 0) & (z - kq >= 0))
        def _():
            use(z - kq)

        @pl.when((q >= 0) & (z + kq < nz))
        def _():
            use(z + kq)

        return 0

    lax.fori_loop(0, rounds + 1, turn, 0)

    for g in range(2):
        own = pl.ds(g * group, group)
        stat_send[g, 0, 0:group] = top[own]
        stat_send[g, 1, 0:group] = tot[own]
        stat_send[g, 2, 0:group] = tgt[own]

    offsets = [(dy, d) for dy in range(2) for d in range(nv) if dy or d]

    def stats(dy, d):
        return pltpu.make_async_remote_copy(
            src_ref=stat_send.at[dy],
            dst_ref=stat_recv.at[dy * nv + d],
            send_sem=st_send.at[dy * nv + d],
            recv_sem=st_recv.at[dy * nv + d],
            device_id=(across if dy else me, (v + d) % nv),
            device_id_type=MESH,
        )

    for dy, d in offsets:
        stats(dy, d).start()

    spread = jnp.zeros((group, tokens), jnp.float32)
    lane = lax.broadcasted_iota(jnp.int32, (group, tokens), 1)
    members = member_ref[...].astype(jnp.float32)
    for e in range(members.shape[1]):
        spread = jnp.where(lane // seq == e, 1.0 - members[:, e : e + 1], spread)
    outside = spread

    own = pl.ds(0, group)
    highest, summed, target_logit = top[own], tot[own], tgt[own]
    for dy, d in offsets:
        stats(dy, d).wait_recv()
        slot = dy * nv + d
        theirs = stat_recv[slot, 0, 0:group]
        raised = jnp.maximum(highest, theirs)
        summed = summed * jnp.exp(highest - raised) + stat_recv[slot, 1, 0:group] * jnp.exp(
            theirs - raised
        )
        highest = raised
        target_logit = target_logit + stat_recv[slot, 2, 0:group]
    confidence = target_logit - (highest + jnp.log(summed))
    weighted = outside * confidence

    mom_send[0:1] = jnp.sum(weighted, axis=0, keepdims=True)
    mom_send[1:2] = jnp.sum(weighted * confidence, axis=0, keepdims=True)

    def moments(d):
        return pltpu.make_async_remote_copy(
            src_ref=mom_send,
            dst_ref=mom_recv.at[d],
            send_sem=mo_send.at[d],
            recv_sem=mo_recv.at[d],
            device_id=((me + d) % nsh, v),
            device_id_type=MESH,
        )

    for d in range(1, nsh):
        moments(d).start()
    total = mom_send[0:2]
    for d in range(1, nsh):
        moments(d).wait_recv()
        total = total + mom_recv[d, 0:2]
    first_moment, second_moment = total[0:1], total[1:2]
    out_count = (group * nsh) // 2 - outside
    out_mean = (first_moment - weighted) / out_count
    out_variance = (second_moment - weighted * confidence) / out_count - out_mean * out_mean
    score = (confidence - out_mean) * lax.rsqrt(jnp.maximum(out_variance, 0.0) + VAR_FLOOR)
    keep = tokens // nv
    shifted = pltpu.roll(score, (nv - v) % nv * keep, 1)
    out_ref[...] = shifted[:, 0:keep]

    def drain(block, _):
        for j in range(chunks):
            side(block, j, c).wait_send()

            @pl.when((block <= z) & has_up)
            def _():
                line(block, j, up_send, me).wait_send()

            @pl.when((block >= z) & has_down)
            def _():
                line(block, j, down_send, me).wait_send()

        return 0

    lax.fori_loop(0, nz, drain, 0)
    for i in range(hparts):
        over_y(i).wait_send()
        for d in range(1, nv):
            over_x(d, i, v).wait_send()
    for dy, d in offsets:
        stats(dy, d).wait_send()
    for d in range(1, nsh):
        moments(d).wait_send()


def per_device(nsh, nv, hidden, targets, membership, unembedding):
    group, tokens, width = hidden.shape
    head_rows = unembedding.shape[0]
    rows = group * tokens
    nz = nsh // 4
    chunks = HEAD_CHUNKS
    hparts = max(1, min(HIDDEN_CHUNKS, rows // nv // 16))
    dma = pltpu.SemaphoreType.DMA
    hbm, vmem = pl.BlockSpec(memory_space=pl.ANY), pl.BlockSpec(memory_space=pltpu.VMEM)
    return pl.pallas_call(
        functools.partial(kernel, nsh, nv, SEQ),
        out_shape=jax.ShapeDtypeStruct((group, tokens // nv), jnp.float32),
        in_specs=[hbm, vmem, vmem, hbm],
        out_specs=vmem,
        scratch_shapes=[
            pltpu.VMEM((2, rows, width), jnp.bfloat16),
            pltpu.VMEM((nz, chunks, 2, head_rows // chunks, width), jnp.bfloat16),
            pltpu.VMEM((2 * group, tokens), jnp.float32),
            pltpu.VMEM((2 * group, tokens), jnp.float32),
            pltpu.VMEM((2 * group, tokens), jnp.float32),
            pltpu.VMEM((2, 3, 8, tokens), jnp.float32),
            pltpu.VMEM((2 * nv, 3, 8, tokens), jnp.float32),
            pltpu.VMEM((8, tokens), jnp.float32),
            pltpu.VMEM((nsh, 8, tokens), jnp.float32),
            dma((chunks + 1,)),
            dma((nz, chunks)),
            dma((nz, chunks)),
            dma((nz, chunks)),
            dma((nz, chunks)),
            dma((nz, chunks)),
            dma((hparts,)),
            dma((hparts,)),
            dma((max(1, nv - 1), hparts)),
            dma((max(1, nv - 1), hparts)),
            dma((2 * nv,)),
            dma((2 * nv,)),
            dma((nsh,)),
            dma((nsh,)),
        ],
        compiler_params=pltpu.CompilerParams(
            collective_id=0, has_side_effects=True, vmem_limit_bytes=48 * 1024 * 1024
        ),
    )(hidden.reshape(rows, width), targets.reshape(1, tokens), membership, unembedding)


def solution(mesh):
    nsh, nv = mesh.shape["shadow"], mesh.shape["vocab"]
    return jax.shard_map(
        functools.partial(per_device, nsh, nv),
        mesh=mesh,
        in_specs=(P("shadow", None, None), P(), P("shadow", None), P(("shadow", "vocab"), None)),
        out_specs=P("shadow", "vocab"),
        check_vma=False,
    )
```

time: 146 us -> 59.1 us (0.40)
  waiting for transfers between devices: 78.5 us -> 0 us
  Pallas kernels: 0 us -> 54.3 us
  blocking collectives: 42.6 us -> 0 us
  between operations: 13.4 us -> 0.01 us
  matrix products: 7.11 us -> 0 us
  local copies, waits for them, and re-layouts: 1.5 us -> 4.55 us
  other arithmetic: 2.67 us -> 0 us
    all_gather x1 -> x0, waiting for transfers between devices: 77.8 us -> none  [per_device(): block_rows = lax.all_gather(unembedding, 'shadow', axis=0, tiled=True)]
    pallas_call x0 -> x1, Pallas kernels: none -> 54.3 us  [per_device(): pl.pallas_call(functools.partial(kernel, nsh, nv, SEQ), out_shape=jax.Sha...]
    psum x1 -> x0, blocking collectives: 29.5 us -> none  [per_device(): lax.psum((jnp.sum(weighted, axis=0), jnp.sum(weighted * confidence, axis=...]
    all_gather x3 -> x0, blocking collectives: 13.1 us -> none  [merged(): everything = jax.tree.map(lambda part: lax.all_gather(part, axis), value)]
    dot_general x1 -> x0, matrix products: 7.11 us -> none  [fold_block(): lax.dot_general(flat_rows, block_rows, (((1,), (1,)), ((), ())), preferre...]
    unnamed x2 -> x9, local copies, waits for them, and re-layouts: 0.01 us -> 4.55 us
    reduce_sum x2 -> x0, other arithmetic: 1.96 us -> none  [the longest x1 1.87 us: fold_block(): summed = jnp.sum(fresh_terms, axis=1)]
  transfers between devices with their start and end apart: 1 -> 0, of which waited for: 1 -> 0; matrix products, arithmetic and copies ran while one was open for 1% -> 0% of each run, Pallas kernels for 0% -> 0%
where the time goes in v1:
time: 59.1 us; the launch traced here: 58.9 us
  Pallas kernels  54.3 us (92%)
  local copies, waits for them, and re-layouts  4.55 us (8%)
    pallas_call x1, Pallas kernels, per_device(): pl.pallas_call(functools.partial(kernel, nsh, nv, SEQ), out_shape=jax.Sha...  54.3 us
    unnamed x9, local copies, waits for them, and re-layouts  4.55 us

profile of v1, /device:TPU:0, one launch (start us, length us, event | category | flops | bytes accessed | tf_op | source)
XLA Modules:
  0.0 58.9 jit_solution(12761946848533879357)
XLA Ops:
  0.0 0.0 copy-start
  0.0 1.6 %copy-done = bf16[4,128,2048]{2,1,0:T(8,128)(2,1)S(1)} copy-done((bf16[4,128,2048]{2,1,0:T(8,128)(2,1)S(1)}, bf16[4,128,2048]{2,1,0:T(8,128)(2,1)}, u32[]{:S(2)}) %copy-start) | copy-done | bytes 2097176
  1.6 0.0 copy-start.1
  1.6 1.0 %copy-done.1 = bf16[128,2048]{1,0:T(8,128)(2,1)S(1)} copy-done((bf16[128,2048]{1,0:T(8,128)(2,1)S(1)}, bf16[128,2048]{1,0:T(8,128)(2,1)}, u32[]{:S(2)}) %copy-start.1) | copy-done | bytes 524312
  2.6 0.0 copy-start.2
  2.6 0.7 %copy-done.2 = s32[4,4]{1,0:T(4,128)S(1)} copy-done((s32[4,4]{1,0:T(4,128)S(1)}, s32[4,4]{1,0:T(4,128)}, u32[]{:S(2)}) %copy-start.2) | copy-done | bytes 88
  3.3 0.0 copy-start.3
  3.3 0.7 %copy-done.3 = s32[128]{0:T(128)S(1)} copy-done((s32[128]{0:T(128)S(1)}, s32[128]{0:T(128)}, u32[]{:S(2)}) %copy-start.3) | copy-done | bytes 536
  4.0 54.3 %shard_map.46 = f32[4,64]{1,0:T(4,128)S(1)} custom-call(bf16[512,2048]{1,0:T(8,128)(2,1)S(1)} %bitcast.2, s32[1,128]{1,0:T(1,128)S(1)} %bitcast.3, s32[4,4]{1,0:T(4,128)S(1)} %copy-done.2, bf16[128,2048]{1,0:T(8,128)(2,1)S(1)} %copy-done.1), custom_call_target="tpu_custom_call" | custom-call | tf_op jit(solution)/shard_map/pallas_call | solution.py:379
  58.3 0.6 copy.6
Async XLA Ops:
  0.0 1.6 %copy-start = (bf16[4,128,2048]{2,1,0:T(8,128)(2,1)S(1)}, bf16[4,128,2048]{2,1,0:T(8,128)(2,1)}, u32[]{:S(2)}) copy-start(bf16[4,128,2048]{2,1,0:T(8,128)(2,1)} %param.4) | copy-start | bytes 6291460
  1.6 1.0 %copy-start.1 = (bf16[128,2048]{1,0:T(8,128)(2,1)S(1)}, bf16[128,2048]{1,0:T(8,128)(2,1)}, u32[]{:S(2)}) copy-start(bf16[128,2048]{1,0:T(8,128)(2,1)} %head_hbm.1) | copy-start | bytes 1572868
  2.6 0.7 %copy-start.2 = (s32[4,4]{1,0:T(4,128)S(1)}, s32[4,4]{1,0:T(4,128)}, u32[]{:S(2)}) copy-start(s32[4,4]{1,0:T(4,128)} %member_ref.1) | copy-start | bytes 196
  3.3 0.7 %copy-start.3 = (s32[128]{0:T(128)S(1)}, s32[128]{0:T(128)}, u32[]{:S(2)}) copy-start(s32[128]{0:T(128)} %param.5) | copy-start | bytes 1540

commit v2 on v1

v2 whole, which is shorter than its diff:
```python
import functools

import jax
import jax.numpy as jnp
from jax import lax
from jax.experimental import pallas as pl
from jax.experimental.pallas import tpu as pltpu
from jax.sharding import PartitionSpec as P

SEQ = 32
NEG_FILL = -1e30
VAR_FLOOR = 0.5
MESH = pl.DeviceIdType.MESH

HEAD_CHUNKS = 8
HIDDEN_CHUNKS = 8


def kernel(
    nsh,
    nv,
    seq,
    hidden_hbm,
    targets_hbm,
    member_hbm,
    head_hbm,
    out_ref,
    targets_ref,
    member_ref,
    hid,
    heads,
    top,
    tot,
    tgt,
    acc,
    outs,
    stat_send,
    stat_recv,
    mom_send,
    mom_recv,
    load_sem,
    up_send,
    down_send,
    line_recv,
    sib_send,
    sib_recv,
    hy_send,
    hy_recv,
    hx_send,
    hx_recv,
    st_send,
    st_recv,
    mo_send,
    mo_recv,
    ou_send,
    ou_recv,
):
    nz = nsh // 4
    chunks, head_rows, slab = heads.shape[1], heads.shape[3], heads.shape[4]
    rows = hid.shape[1]
    tokens = targets_ref.shape[1]
    group = rows // tokens
    piece = rows // nv
    hparts = hy_send.shape[0]
    part = piece // hparts

    me = lax.axis_index("shadow")
    v = lax.axis_index("vocab")
    z, y, c = me // 4, (me // 2) % 2, me % 2
    sibling = me + 1 - 2 * c
    across = me + 2 - 4 * y
    has_up, has_down = z + 1 < nz, z >= 1
    one, zero = jnp.int32(1), jnp.int32(0)

    load_head = [
        pltpu.make_async_copy(
            head_hbm.at[:, pl.ds(j * slab, slab)], heads.at[z, j, c], load_sem.at[j]
        )
        for j in range(chunks)
    ]
    load_hidden = pltpu.make_async_copy(hidden_hbm, hid.at[0], load_sem.at[chunks])
    load_small = [
        pltpu.make_async_copy(targets_hbm, targets_ref, load_sem.at[chunks + 1]),
        pltpu.make_async_copy(member_hbm, member_ref, load_sem.at[chunks + 2]),
    ]
    for copy in load_head + [load_hidden] + load_small:
        copy.start()

    barrier = pltpu.get_barrier_semaphore()

    def greet(s, w):
        pl.semaphore_signal(barrier, inc=1, device_id=(s, w), device_id_type=MESH)

    greet(sibling, v)
    greet(across, v)
    for d in range(1, nv):
        greet(me, (v + d) % nv)

    @pl.when(has_up)
    def _():
        greet(me + 4, v)

    @pl.when(has_down)
    def _():
        greet(me - 4, v)

    top[...] = jnp.full_like(top, NEG_FILL)
    tot[...] = jnp.zeros_like(tot)
    tgt[...] = jnp.zeros_like(tgt)
    pl.semaphore_wait(
        barrier, nv + 1 + jnp.where(has_up, one, zero) + jnp.where(has_down, one, zero)
    )

    def line(block, j, send, target):
        return pltpu.make_async_remote_copy(
            src_ref=heads.at[block, j, c],
            dst_ref=heads.at[block, j, c],
            send_sem=send.at[block, j],
            recv_sem=line_recv.at[block, j],
            device_id=(target, v),
            device_id_type=MESH,
        )

    def side(block, j, core):
        return pltpu.make_async_remote_copy(
            src_ref=heads.at[block, j, core],
            dst_ref=heads.at[block, j, core],
            send_sem=sib_send.at[block, j],
            recv_sem=sib_recv.at[block, j],
            device_id=(sibling, v),
            device_id_type=MESH,
        )

    def over_y(i):
        where = pl.ds(pl.multiple_of(v * piece + i * part, part), part)
        return pltpu.make_async_remote_copy(
            src_ref=hid.at[0, where],
            dst_ref=hid.at[1, where],
            send_sem=hy_send.at[i],
            recv_sem=hy_recv.at[i],
            device_id=(across, v),
            device_id_type=MESH,
        )

    def over_x(d, i, owner):
        where = pl.ds(pl.multiple_of(owner * piece + i * part, part), part)
        return pltpu.make_async_remote_copy(
            src_ref=hid.at[1, where],
            dst_ref=hid.at[1, where],
            send_sem=hx_send.at[d - 1, i],
            recv_sem=hx_recv.at[d - 1, i],
            device_id=(me, (v + d) % nv),
            device_id_type=MESH,
        )

    for j in range(chunks):
        load_head[j].wait()

        @pl.when(has_up)
        def _():
            line(z, j, up_send, me + 4).start()

        @pl.when(has_down)
        def _():
            line(z, j, down_send, me - 4).start()

        side(z, j, c).start()
    load_hidden.wait()
    for i in range(hparts):
        over_y(i).start()

    for copy in load_small:
        copy.wait()
    wanted = targets_ref[...]
    lane = lax.broadcasted_iota(jnp.int32, (group, tokens), 1)
    members = member_ref[...].astype(jnp.float32)
    spread = jnp.zeros((group, tokens), jnp.float32)
    for e in range(members.shape[1]):
        spread = jnp.where(lane // seq == e, 1.0 - members[:, e : e + 1], spread)
    outs[0] = spread
    share_outs = pltpu.make_async_remote_copy(
        src_ref=outs.at[0],
        dst_ref=outs.at[1],
        send_sem=ou_send.at[0],
        recv_sem=ou_recv.at[0],
        device_id=(across, v),
        device_id_type=MESH,
    )
    share_outs.start()

    def product(which, block, j):
        words = heads[block, j].reshape(2 * head_rows, slab)
        where = pl.ds(pl.multiple_of(j * slab, slab), slab)
        return lax.dot_general(
            words,
            hid[which, :, where],
            (((1,), (1,)), ((), ())),
            preferred_element_type=jnp.float32,
        )

    def absorb(which, logits, block):
        i = lax.broadcasted_iota(jnp.int32, (2 * head_rows, tokens), 0)
        first = (block * 2 + y) * 2
        ids = ((first + i // head_rows) * nv + v) * head_rows + i % head_rows
        hit = ids == wanted
        for s in range(group):
            row = pl.ds(which * group + s, 1)
            mine = logits[:, s * tokens : (s + 1) * tokens]
            tgt[row] += jnp.sum(jnp.where(hit, mine, 0.0), axis=0, keepdims=True)
            others = jnp.where(hit, NEG_FILL, mine)
            before = top[row]
            raised = jnp.maximum(before, jnp.max(others, axis=0, keepdims=True))
            terms = jnp.sum(jnp.exp(others - raised), axis=0, keepdims=True)
            tot[row] = tot[row] * jnp.exp(before - raised) + terms
            top[row] = raised

    def whole_block(which, block):
        words = jnp.concatenate(
            [heads[block, j].reshape(2 * head_rows, slab) for j in range(chunks)], axis=1
        )
        logits = lax.dot_general(
            words, hid[which], (((1,), (1,)), ((), ())), preferred_element_type=jnp.float32
        )
        absorb(which, logits, block)

    def from_sibling(block):
        def one_wait(j, _):
            side(block, j, 1 - c).wait_recv()
            return 0

        lax.fori_loop(0, chunks, one_wait, 0)

    def fold_step(k):
        @pl.when(z - k >= 0)
        def _():
            from_sibling(z - k)
            whole_block(0, z - k)

        @pl.when((k > 0) & (z + k < nz))
        def _():
            from_sibling(z + k)
            whole_block(0, z + k)

    def arrive(k, j):
        low, high = z - k, z + k

        @pl.when(low >= 0)
        def _():
            line(low, j, up_send, me).wait_recv()

            @pl.when(has_up)
            def _():
                line(low, j, up_send, me + 4).start()

            side(low, j, c).start()

        @pl.when(high < nz)
        def _():
            line(high, j, down_send, me).wait_recv()

            @pl.when(has_down)
            def _():
                line(high, j, down_send, me - 4).start()

            side(high, j, c).start()

    last = nz - 1
    early = (last - 1) * chunks
    pace = max(1, min(2, early // hparts))

    def turn(r, _):
        arrive(1 + r // chunks, r % chunks)

        @pl.when((r % pace == pace - 1) & (r // pace < hparts))
        def _():
            i = r // pace
            over_y(i).wait_recv()
            for d in range(1, nv):
                over_x(d, i, v).start()

        @pl.when(r % chunks == 0)
        def _():
            fold_step(r // chunks)

        return 0

    lax.fori_loop(0, early, turn, 0)

    at_end = (z == 0) | (z == last)
    final = jnp.where(z == 0, jnp.int32(last), zero)
    middle = chunks // 2
    acc[...] = jnp.zeros_like(acc)

    def closing(j, _):
        arrive(last, j)

        @pl.when(j == 0)
        def _():
            fold_step(last - 1)

        @pl.when(j == middle)
        def _():
            for d in range(1, nv):
                for i in range(hparts):
                    over_x(d, i, (v + nv - d) % nv).wait_recv()

            def catch_up(block, _):
                away = jnp.where(block > z, block - z, z - block)

                @pl.when(away < last)
                def _():
                    whole_block(1, block)

                return 0

            lax.fori_loop(0, nz, catch_up, 0)

            @pl.when(at_end)
            def _():
                def missed(i, _):
                    acc[1] += product(1, final, i)
                    return 0

                lax.fori_loop(0, middle - 1, missed, 0)

        @pl.when(at_end & (j >= 1))
        def _():
            side(final, j - 1, 1 - c).wait_recv()
            acc[0] += product(0, final, j - 1)

            @pl.when(j >= middle)
            def _():
                acc[1] += product(1, final, j - 1)

        return 0

    lax.fori_loop(0, chunks, closing, 0)

    @pl.when(at_end)
    def _():
        side(final, chunks - 1, 1 - c).wait_recv()
        for which in range(2):
            absorb(which, acc[which] + product(which, final, chunks - 1), final)

    stat_send[0] = top[...]
    stat_send[1] = tot[...]
    stat_send[2] = tgt[...]

    offsets = [(dy, d) for dy in range(2) for d in range(nv) if dy or d]

    def stats(dy, d):
        return pltpu.make_async_remote_copy(
            src_ref=stat_send,
            dst_ref=stat_recv.at[dy * nv + d],
            send_sem=st_send.at[dy * nv + d],
            recv_sem=st_recv.at[dy * nv + d],
            device_id=(across if dy else me, (v + d) % nv),
            device_id_type=MESH,
        )

    for dy, d in offsets:
        stats(dy, d).start()

    share_outs.wait_recv()
    outside = jnp.concatenate([outs[0], outs[1]], axis=0)

    def seen(slot, which):
        value = stat_recv[slot, which]
        return pltpu.roll(value, group, 0) if slot >= nv else value

    highest, summed, target_logit = top[...], tot[...], tgt[...]
    for dy, d in offsets:
        stats(dy, d).wait_recv()
        slot = dy * nv + d
        theirs = seen(slot, 0)
        raised = jnp.maximum(highest, theirs)
        summed = summed * jnp.exp(highest - raised) + seen(slot, 1) * jnp.exp(theirs - raised)
        highest = raised
        target_logit = target_logit + seen(slot, 2)
    confidence = target_logit - (highest + jnp.log(summed))
    weighted = outside * confidence
    squared = weighted * confidence

    mom_send[0:1] = jnp.sum(weighted, axis=0, keepdims=True)
    mom_send[1:2] = jnp.sum(squared, axis=0, keepdims=True)

    around = [(dz, dc) for dz in range(nz) for dc in range(2) if dz or dc]

    def moments(dz, dc):
        column = (z + dz) % nz * 4 + y * 2 + (c + dc) % 2
        return pltpu.make_async_remote_copy(
            src_ref=mom_send,
            dst_ref=mom_recv.at[2 * dz + dc],
            send_sem=mo_send.at[2 * dz + dc],
            recv_sem=mo_recv.at[2 * dz + dc],
            device_id=(column, v),
            device_id_type=MESH,
        )

    for dz, dc in around:
        moments(dz, dc).start()
    total = mom_send[0:2]
    for dz, dc in around:
        moments(dz, dc).wait_recv()
        total = total + mom_recv[2 * dz + dc, 0:2]
    first_moment, second_moment = total[0:1], total[1:2]
    out_count = (group * nsh) // 2 - outside
    out_mean = (first_moment - weighted) / out_count
    out_variance = (second_moment - squared) / out_count - out_mean * out_mean
    score = (confidence - out_mean) * lax.rsqrt(jnp.maximum(out_variance, 0.0) + VAR_FLOOR)
    keep = tokens // nv
    shifted = pltpu.roll(score, (nv - v) % nv * keep, 1)
    out_ref[...] = shifted[0:group, 0:keep]

    def drain(block, _):
        for j in range(chunks):
            side(block, j, c).wait_send()

            @pl.when((block <= z) & has_up)
            def _():
                line(block, j, up_send, me).wait_send()

            @pl.when((block >= z) & has_down)
            def _():
                line(block, j, down_send, me).wait_send()

        return 0

    lax.fori_loop(0, nz, drain, 0)
    for i in range(hparts):
        over_y(i).wait_send()
        for d in range(1, nv):
            over_x(d, i, v).wait_send()
    for dy, d in offsets:
        stats(dy, d).wait_send()
    for dz, dc in around:
        moments(dz, dc).wait_send()
    share_outs.wait_send()


def per_device(nsh, nv, hidden, targets, membership, unembedding):
    group, tokens, width = hidden.shape
    head_rows = unembedding.shape[0]
    rows = group * tokens
    nz = nsh // 4
    chunks = HEAD_CHUNKS
    hparts = max(1, min(HIDDEN_CHUNKS, rows // nv // 16))
    dma = pltpu.SemaphoreType.DMA
    hbm, vmem = pl.BlockSpec(memory_space=pltpu.HBM), pl.BlockSpec(memory_space=pltpu.VMEM)
    return pl.pallas_call(
        functools.partial(kernel, nsh, nv, SEQ),
        out_shape=jax.ShapeDtypeStruct((group, tokens // nv), jnp.float32),
        in_specs=[hbm] * 4,
        out_specs=vmem,
        scratch_shapes=[
            pltpu.VMEM((1, tokens), jnp.int32),
            pltpu.VMEM(membership.shape, jnp.int32),
            pltpu.VMEM((2, rows, width), jnp.bfloat16),
            pltpu.VMEM((nz, chunks, 2, head_rows, width // chunks), jnp.bfloat16),
            pltpu.VMEM((2 * group, tokens), jnp.float32),
            pltpu.VMEM((2 * group, tokens), jnp.float32),
            pltpu.VMEM((2 * group, tokens), jnp.float32),
            pltpu.VMEM((2, 2 * head_rows, rows), jnp.float32),
            pltpu.VMEM((2, group, tokens), jnp.float32),
            pltpu.VMEM((3, 2 * group, tokens), jnp.float32),
            pltpu.VMEM((2 * nv, 3, 2 * group, tokens), jnp.float32),
            pltpu.VMEM((8, tokens), jnp.float32),
            pltpu.VMEM((2 * nz, 8, tokens), jnp.float32),
            dma((chunks + 3,)),
            dma((nz, chunks)),
            dma((nz, chunks)),
            dma((nz, chunks)),
            dma((nz, chunks)),
            dma((nz, chunks)),
            dma((hparts,)),
            dma((hparts,)),
            dma((max(1, nv - 1), hparts)),
            dma((max(1, nv - 1), hparts)),
            dma((2 * nv,)),
            dma((2 * nv,)),
            dma((2 * nz,)),
            dma((2 * nz,)),
            dma((1,)),
            dma((1,)),
        ],
        compiler_params=pltpu.CompilerParams(
            collective_id=0, has_side_effects=True, vmem_limit_bytes=67043328
        ),
    )(hidden.reshape(rows, width), targets.reshape(1, tokens), membership, unembedding)


def solution(mesh):
    nsh, nv = mesh.shape["shadow"], mesh.shape["vocab"]
    return jax.shard_map(
        functools.partial(per_device, nsh, nv),
        mesh=mesh,
        in_specs=(P("shadow", None, None), P(), P("shadow", None), P(("shadow", "vocab"), None)),
        out_specs=P("shadow", "vocab"),
        check_vma=False,
    )
```

time: 59.1 us -> 55.4 us (0.937)
  local copies, waits for them, and re-layouts: 4.55 us -> 1.26 us
    unnamed x9 -> x1, local copies, waits for them, and re-layouts: 4.55 us -> 1.26 us
where the time goes in v2:
time: 55.4 us; the launch traced here: 55.3 us
  Pallas kernels  54 us (97%)
  local copies, waits for them, and re-layouts  1.26 us (2%)
    pallas_call x1, Pallas kernels, per_device(): pl.pallas_call(functools.partial(kernel, nsh, nv, SEQ), out_shape=jax.Sha...  54 us
    unnamed x1, local copies, waits for them, and re-layouts  1.26 us

profile of v2, /device:TPU:0, one launch (start us, length us, event | category | flops | bytes accessed | tf_op | source)
XLA Modules:
  0.0 55.3 jit_solution(14605054152049280000)
XLA Ops:
  0.0 54.0 %shard_map.46 = f32[4,64]{1,0:T(4,128)} custom-call(bf16[512,2048]{1,0:T(8,128)(2,1)} %bitcast.2, s32[1,128]{1,0:T(1,128)} %bitcast.3, s32[4,4]{1,0:T(4,128)} %member_hbm.1, bf16[128,2048]{1,0:T(8,128)(2,1)} %head_hbm.1), custom_call_target="tpu_custom_call" | custom-call | tf_op jit(solution)/shard_map/pallas_call | solution.py:450
  54.0 1.3 %copy.6 = f32[4,64]{1,0:T(4,128)} copy(f32[4,64]{1,0:T(4,128)} %shard_map.46) | data formatting | bytes 2048

commit v3 on v2

--- a/solution.py
+++ b/solution.py
@@ -12,7 +12,7 @@
 VAR_FLOOR = 0.5
 MESH = pl.DeviceIdType.MESH
 
-HEAD_CHUNKS = 8
+HEAD_CHUNKS = 4
 HIDDEN_CHUNKS = 8
 
 
@@ -56,7 +56,7 @@
     ou_recv,
 ):
     nz = nsh // 4
-    chunks, head_rows, slab = heads.shape[1], heads.shape[3], heads.shape[4]
+    chunks, head_rows, slab = heads.shape[0], heads.shape[3], heads.shape[4]
     rows = hid.shape[1]
     tokens = targets_ref.shape[1]
     group = rows // tokens
@@ -74,7 +74,7 @@
 
     load_head = [
         pltpu.make_async_copy(
-            head_hbm.at[:, pl.ds(j * slab, slab)], heads.at[z, j, c], load_sem.at[j]
+            head_hbm.at[:, pl.ds(j * slab, slab)], heads.at[j, z, c], load_sem.at[j]
         )
         for j in range(chunks)
     ]
@@ -113,8 +113,8 @@
 
     def line(block, j, send, target):
         return pltpu.make_async_remote_copy(
-            src_ref=heads.at[block, j, c],
-            dst_ref=heads.at[block, j, c],
+            src_ref=heads.at[j, block, c],
+            dst_ref=heads.at[j, block, c],
             send_sem=send.at[block, j],
             recv_sem=line_recv.at[block, j],
             device_id=(target, v),
@@ -123,8 +123,8 @@
 
     def side(block, j, core):
         return pltpu.make_async_remote_copy(
-            src_ref=heads.at[block, j, core],
-            dst_ref=heads.at[block, j, core],
+            src_ref=heads.at[j, block, core],
+            dst_ref=heads.at[j, block, core],
             send_sem=sib_send.at[block, j],
             recv_sem=sib_recv.at[block, j],
             device_id=(sibling, v),
@@ -189,7 +189,7 @@
     share_outs.start()
 
     def product(which, block, j):
-        words = heads[block, j].reshape(2 * head_rows, slab)
+        words = heads[j, block].reshape(2 * head_rows, slab)
         where = pl.ds(pl.multiple_of(j * slab, slab), slab)
         return lax.dot_general(
             words,
@@ -198,13 +198,14 @@
             preferred_element_type=jnp.float32,
         )
 
-    def absorb(which, logits, block):
-        i = lax.broadcasted_iota(jnp.int32, (2 * head_rows, tokens), 0)
-        first = (block * 2 + y) * 2
-        ids = ((first + i // head_rows) * nv + v) * head_rows + i % head_rows
+    def absorb(row0, logits, block):
+        count = logits.shape[0]
+        i = lax.broadcasted_iota(jnp.int32, (count, tokens), 0)
+        first = (block + i // (2 * head_rows)) * 4 + y * 2 + i // head_rows % 2
+        ids = (first * nv + v) * head_rows + i % head_rows
         hit = ids == wanted
-        for s in range(group):
-            row = pl.ds(which * group + s, 1)
+        for s in range(logits.shape[1] // tokens):
+            row = pl.ds(row0 + s, 1)
             mine = logits[:, s * tokens : (s + 1) * tokens]
             tgt[row] += jnp.sum(jnp.where(hit, mine, 0.0), axis=0, keepdims=True)
             others = jnp.where(hit, NEG_FILL, mine)
@@ -214,14 +215,24 @@
             tot[row] = tot[row] * jnp.exp(before - raised) + terms
             top[row] = raised
 
+    def fold_blocks(block, count, which, start, size):
+        words = jnp.concatenate(
+            [
+                heads[j, pl.ds(block, count)].reshape(count * 2 * head_rows, slab)
+                for j in range(chunks)
+            ],
+            axis=1,
+        )
+        logits = lax.dot_general(
+            words,
+            hid[which, pl.ds(start, size)],
+            (((1,), (1,)), ((), ())),
+            preferred_element_type=jnp.float32,
+        )
+        absorb(which * group + start // tokens, logits, block)
+
     def whole_block(which, block):
-        words = jnp.concatenate(
-            [heads[block, j].reshape(2 * head_rows, slab) for j in range(chunks)], axis=1
-        )
-        logits = lax.dot_general(
-            words, hid[which], (((1,), (1,)), ((), ())), preferred_element_type=jnp.float32
-        )
-        absorb(which, logits, block)
+        fold_blocks(block, 1, which, 0, rows)
 
     def from_sibling(block):
         def one_wait(j, _):
@@ -289,6 +300,9 @@
     at_end = (z == 0) | (z == last)
     final = jnp.where(z == 0, jnp.int32(last), zero)
     middle = chunks // 2
+    by_piece = piece % tokens == 0
+    unit = piece if by_piece else rows
+    base = jnp.where(z == last, one, zero)
     acc[...] = jnp.zeros_like(acc)
 
     def closing(j, _):
@@ -297,23 +311,30 @@
         @pl.when(j == 0)
         def _():
             fold_step(last - 1)
+
+        def catch_up(owner):
+            start = pl.multiple_of(owner * unit, unit)
+            fold_blocks(base, last, 1, start, unit)
+
+            @pl.when(jnp.logical_not(at_end))
+            def _():
+                fold_blocks(last, 1, 1, start, unit)
+
+        if by_piece:
+
+            @pl.when(j == 0)
+            def _():
+                catch_up(v)
 
         @pl.when(j == middle)
         def _():
             for d in range(1, nv):
                 for i in range(hparts):
                     over_x(d, i, (v + nv - d) % nv).wait_recv()
-
-            def catch_up(block, _):
-                away = jnp.where(block > z, block - z, z - block)
-
-                @pl.when(away < last)
-                def _():
-                    whole_block(1, block)
-
-                return 0
-
-            lax.fori_loop(0, nz, catch_up, 0)
+                if by_piece:
+                    catch_up((v + nv - d) % nv)
+            if not by_piece:
+                catch_up(zero)
 
             @pl.when(at_end)
             def _():
@@ -340,7 +361,7 @@
     def _():
         side(final, chunks - 1, 1 - c).wait_recv()
         for which in range(2):
-            absorb(which, acc[which] + product(which, final, chunks - 1), final)
+            absorb(which * group, acc[which] + product(which, final, chunks - 1), final)
 
     stat_send[0] = top[...]
     stat_send[1] = tot[...]
@@ -456,7 +477,7 @@
             pltpu.VMEM((1, tokens), jnp.int32),
             pltpu.VMEM(membership.shape, jnp.int32),
             pltpu.VMEM((2, rows, width), jnp.bfloat16),
-            pltpu.VMEM((nz, chunks, 2, head_rows, width // chunks), jnp.bfloat16),
+            pltpu.VMEM((chunks, nz, 2, head_rows, width // chunks), jnp.bfloat16),
             pltpu.VMEM((2 * group, tokens), jnp.float32),
             pltpu.VMEM((2 * group, tokens), jnp.float32),
             pltpu.VMEM((2 * group, tokens), jnp.float32),

time: 55.4 us -> 52.8 us (0.953)
  Pallas kernels: 54 us -> 51.4 us
    pallas_call x1, Pallas kernels: 54 us -> 51.4 us  [per_device(): pl.pallas_call(functools.partial(kernel, nsh, nv, SEQ), out_shape=jax.Sha...]
where the time goes in v3:
time: 52.8 us; the launch traced here: 52.6 us
  Pallas kernels  51.4 us (97%)
  local copies, waits for them, and re-layouts  1.26 us (2%)
    pallas_call x1, Pallas kernels, per_device(): pl.pallas_call(functools.partial(kernel, nsh, nv, SEQ), out_shape=jax.Sha...  51.4 us
    unnamed x1, local copies, waits for them, and re-layouts  1.26 us

profile of v3, /device:TPU:0, one launch (start us, length us, event | category | flops | bytes accessed | tf_op | source)
XLA Modules:
  0.0 52.6 jit_solution(14569866340084020582)
XLA Ops:
  0.0 51.4 %shard_map.46 = f32[4,64]{1,0:T(4,128)} custom-call(bf16[512,2048]{1,0:T(8,128)(2,1)} %bitcast.2, s32[1,128]{1,0:T(1,128)} %bitcast.3, s32[4,4]{1,0:T(4,128)} %member_hbm.1, bf16[128,2048]{1,0:T(8,128)(2,1)} %head_hbm.1), custom_call_target="tpu_custom_call" | custom-call | tf_op jit(solution)/shard_map/pallas_call | solution.py:471
  51.4 1.3 %copy.6 = f32[4,64]{1,0:T(4,128)} copy(f32[4,64]{1,0:T(4,128)} %shard_map.46) | data formatting | bytes 2048
